TPU v7x, 32 devices: a whole 2x2x4 slice. The times are simulated.
32 devices in a mesh: grp: 4 (over y, x), dev: 8 (over z, core).
Axes of the slice: x: 2, y: 2, z: 4, core: 2. Of those that a mesh axis runs over, the one named last changes fastest.
Arguments:
- table: float32 [262144, 128], P(('grp', 'dev')), may hold values from -6 to 6
- cold_grads: float32 [131072, 128], P(('grp', 'dev')), may hold values from -6 to 6
- cold_owner: int32 [131072, 1], P(('grp', 'dev')), may hold values from 0 to 31; in each aligned block of 4096 rows (0 to 4095, 4096 to 8191, ...) at most 256 rows name the same one
- cold_row: int32 [131072], P(('grp', 'dev')), may hold values from 0 to 8191
- hot_grads: float32 [32768, 128], P(('grp', 'dev')), may hold values from -6 to 6
- hot_slot: int32 [32768], P(('grp', 'dev')), may hold values from 0 to 255
- hot_ids: int32 [256], replicated, may hold values from 0 to 262143, as said below
Outputs:
- new_table: float32 [262144, 128], P(('grp', 'dev'))
Inputs may be any that keep to these rules, and one draw needn't show every extreme that they name: `cold_owner`: among the 4096 rare-row lookups of one device no owner is named more than 256 times, a bound that some block reaches. `hot_ids`: all entries differ.
All inputs are finite; a program needn't handle non-finite values.
Results may differ from a plain program's by a relative error of at most 0.00005.
Values sent between devices are 32-bit elements; how exact they have to be, the bound alone decides.
A program may use at most 64 MiB of HBM per device.

v0:
```python
import jax
import jax.numpy as jnp
from jax import lax
from jax.sharding import PartitionSpec as P

LEARN = 0.05


def hot_update(table, hot_grads, hot_slot, hot_ids):
    count = hot_ids.shape[0]
    pick = (jnp.arange(count, dtype=jnp.int32)[:, None] == hot_slot[None, :]).astype(jnp.float32)
    partial_sum = jnp.dot(
        pick, hot_grads, precision=lax.Precision.HIGHEST, preferred_element_type=jnp.float32
    )
    share = lax.psum_scatter(partial_sum, "dev", scatter_dimension=0, tiled=True)
    share = lax.psum(share, "grp")
    total = lax.all_gather(share, "dev", axis=0, tiled=True)
    rows_dev = table.shape[0]
    local = hot_ids - lax.axis_index(("grp", "dev")) * rows_dev
    inside = (local >= 0) & (local < rows_dev)
    target = jnp.where(inside, local, rows_dev)
    return table.at[target].add(-LEARN * total, mode="drop")


def pack_cold(cold_grads, cold_owner, cold_row, devices, slots):
    owner = cold_owner[:, 0]
    onehot = (owner[:, None] == jnp.arange(devices, dtype=jnp.int32)[None, :]).astype(jnp.int32)
    running = jnp.cumsum(onehot, axis=0) - 1
    rank = jnp.sum(running * onehot, axis=1)
    target = owner * slots + rank
    width = cold_grads.shape[1]
    send_grads = jnp.zeros((devices * slots, width), jnp.float32).at[target].set(cold_grads)
    send_rows = jnp.zeros((devices * slots,), jnp.int32).at[target].set(cold_row)
    return (send_grads, send_rows)


def on_device(table, cold_grads, cold_owner, cold_row, hot_grads, hot_slot, hot_ids):
    n_grp = lax.axis_size("grp")
    n_dev = lax.axis_size("dev")
    devices = n_grp * n_dev
    width = table.shape[1]
    slots = max(4, 2 * cold_grads.shape[0] // devices)
    send_grads, send_rows = pack_cold(cold_grads, cold_owner, cold_row, devices, slots)
    grads_four = send_grads.reshape(n_grp, n_dev, slots, width)
    rows_three = send_rows.reshape(n_grp, n_dev, slots)
    got_grads, got_rows = (
        lax.all_to_all(
            lax.all_to_all(grads_four, "grp", split_axis=0, concat_axis=0, tiled=True),
            "dev",
            split_axis=1,
            concat_axis=1,
            tiled=True,
        ),
        lax.all_to_all(
            lax.all_to_all(rows_three, "grp", split_axis=0, concat_axis=0, tiled=True),
            "dev",
            split_axis=1,
            concat_axis=1,
            tiled=True,
        ),
    )
    current = hot_update(table, hot_grads, hot_slot, hot_ids)
    current = current.at[got_rows.reshape(-1)].add(-LEARN * got_grads.reshape(-1, width))
    return current


def solution(mesh):
    in_specs = (
        P(("grp", "dev"), None),
        P(("grp", "dev"), None),
        P(("grp", "dev"), None),
        P(("grp", "dev")),
        P(("grp", "dev"), None),
        P(("grp", "dev")),
        P(),
    )
    out_specs = P(("grp", "dev"), None)
    return jax.shard_map(
        on_device, mesh=mesh, in_specs=in_specs, out_specs=out_specs, check_vma=False
    )
```

profile of v0, /device:TPU:4, one launch (start us, length us, event | category | flops | bytes accessed | tf_op | source)
XLA Modules:
  0.0 298.4 jit_solution(3252168921994145079)
XLA Ops:
  6.5 0.0 copy-start
  6.5 0.0 copy-start.1
  6.5 4.5 %copy.23 = f32[8192,128]{1,0:T(8,128)} copy(f32[8192,128]{1,0:T(8,128)} %param.7) | data formatting | bytes 8388608
  11.1 0.0 copy-done.1
  11.1 0.1 fusion.6
  11.1 9.2 %reduce-window.6 = s32[32,32,128]{2,1,0:T(8,128)S(1)} reduce-window(s32[32,32,128]{2,1,0:T(8,128)S(1)} %fusion.6, s32[]{:T(128)} %constant.13.clone.1), window={size=1x1x128 pad=0_0x0_0x127_0}, to_apply=%region_3.4 | reduce-window | flops 16646144 | bytes 1048580 | tf_op jit(solution)/shard_map/reduce-window
  20.4 0.8 slice_reduce_fusion
  21.2 0.2 reduce-window.9
  21.4 0.2 add_add_fusion
  21.6 0.3 fusion.4
  21.9 15.7 %scatter_custom_fusion.1 = s32[8192]{0:T(1024)S(1)} fusion(s32[4096]{0:T(1024)S(1)} %bitcast.30, s32[4096]{0:T(1024)} %param.10, s32[]{:T(128)} %constant.13.clone.1), kind=kCustom, calls=%fused_computation.23 | custom fusion | bytes 33280 | tf_op jit(solution)/shard_map/scatter | solution.py:33
  37.7 0.6 reshape.61
  38.3 4.2 %all-to-all-start = ((s32[4,8,256]{2,1,0:T(8,128)}), s32[4,8,256]{2,1,0:T(8,128)S(1)}, u32[]{:S(2)}, u32[]{:S(2)}) async-start(s32[4,8,256]{2,1,0:T(8,128)} %reshape.61), calls=%async_computation.1 | async-start | bytes 65536 | tf_op jit(solution)/shard_map/all_to_all | solution.py:55
  42.5 13.1 %scatter_custom_fusion.2 = f32[8192,128]{1,0:T(8,128)} fusion(s32[4096]{0:T(1024)S(1)} %bitcast.31, f32[4096,128]{1,0:T(8,128)} %param.8, f32[]{:T(128)} %constant.17.clone.1), kind=kCustom, calls=%fused_computation.5 | custom fusion | bytes 4194816 | tf_op jit(solution)/shard_map/scatter | solution.py:32
  55.6 0.0 all-to-all-done
  55.6 4.9 %all-to-all-start.2 = ((f32[4,8,256,128]{3,2,1,0:T(8,128)}), f32[4,8,256,128]{3,2,1,0:T(8,128)}, u32[]{:S(2)}, u32[]{:S(2)}) async-start(f32[4,8,256,128]{3,2,1,0:T(8,128)} %bitcast.23), calls=%async_computation.3 | async-start | bytes 8388608 | tf_op jit(solution)/shard_map/all_to_all | solution.py:48
  60.4 0.6 copy.13
  61.0 46.2 %all-to-all-done.2 = f32[4,8,256,128]{3,2,1,0:T(8,128)} async-done(((f32[4,8,256,128]{3,2,1,0:T(8,128)}), f32[4,8,256,128]{3,2,1,0:T(8,128)}, u32[]{:S(2)}, u32[]{:S(2)}) %all-to-all-start.2) | async-done | bytes 4194336 | tf_op jit(solution)/shard_map/all_to_all | solution.py:48
  107.3 4.9 %all-to-all-start.1 = ((s32[4,8,256]{2,0,1:T(4,128)}), s32[4,8,256]{2,0,1:T(4,128)S(1)}, u32[]{:S(2)}, u32[]{:S(2)}) async-start(s32[4,8,256]{2,0,1:T(4,128)} %copy.13), calls=%async_computation.2 | async-start | bytes 65536 | tf_op jit(solution)/shard_map/all_to_all | solution.py:54
  112.1 4.6 %copy.15 = f32[4,8,256,128]{3,2,0,1:T(8,128)} copy(f32[4,8,256,128]{3,2,1,0:T(8,128)} %all-to-all-done.2) | data formatting | bytes 8388608 | tf_op jit(solution)/shard_map/all_to_all | solution.py:48
  116.7 0.0 copy-start.2
  116.7 0.0 copy-start.3
  116.7 1.2 all-to-all-done.1
  117.9 4.5 %all-to-all-start.3 = ((f32[4,8,256,128]{3,2,0,1:T(8,128)}), f32[4,8,256,128]{3,2,0,1:T(8,128)}, u32[]{:S(2)}, u32[]{:S(2)}) async-start(f32[4,8,256,128]{3,2,0,1:T(8,128)} %copy.15), calls=%async_computation.4 | async-start | bytes 8388608 | tf_op jit(solution)/shard_map/all_to_all | solution.py:47
  122.4 0.0 reduce-scatter.2.cloned.1.call-start
  122.5 0.0 copy-done
  122.5 0.0 copy-done.2
  122.5 1.3 fusion.2
  123.8 0.0 reduce-scatter.2.cloned.1.call-update
  123.9 0.0 copy-done.3
  124.0 33.3 %reduce-scatter.2.cloned.1.call-done = f32[32,128]{1,0:T(8,128)} async-done(((f32[256,128]{1,0:T(8,128)}), f32[32,128]{1,0:T(8,128)}) %reduce-scatter.2.cloned.1.call-update) | async-done | bytes 16400 | tf_op jit(solution)/shard_map/reduce_scatter | solution.py:15
  157.3 15.7 %psum.7 = f32[32,128]{1,0:T(8,128)S(1)} all-reduce(f32[32,128]{1,0:T(8,128)} %reduce-scatter.2.cloned.1.call-done), channel_id=1, replica_groups=mesh['grp'=4,'dev'=8] {'grp'}, use_global_device_ids=true, to_apply=%region_1.2 | all-reduce | flops 4096 | bytes 32768 | tf_op jit(solution)/shard_map/psum | solution.py:16
  172.9 50.9 %all_gather.3 = f32[256,128]{1,0:T(8,128)S(1)} all-gather(f32[32,128]{1,0:T(8,128)S(1)} %psum.7), channel_id=1, replica_groups=mesh['grp'=4,'dev'=8] {'dev'}, dimensions={0}, use_global_device_ids=true | all-gather | bytes 147456 | tf_op jit(solution)/shard_map/all_gather | solution.py:17
  223.9 6.0 %scatter_custom_fusion = f32[8192,128]{1,0:T(8,128)} fusion(f32[8192,128]{1,0:T(8,128)} %copy.23, s32[256]{0:T(256)S(1)} %compare_select_fusion.2, f32[256,128]{1,0:T(8,128)S(1)} %all_gather.3, f32[]{:T(128)} %constant.14.clone.1), kind=kCustom, calls=%fused_computation.19 | custom fusion | flops 65536 | bytes 4325888 | tf_op jit(solution)/shard_map/scatter-add | solution.py:22
  229.9 0.0 all-to-all-done.3
  229.9 4.7 %copy_multiply_fusion = f32[4,8,256,128]{3,2,1,0:T(8,128)} fusion(f32[4,8,256,128]{3,2,0,1:T(8,128)} %all-to-all-done.3), kind=kLoop, calls=%fused_computation.4 | loop fusion | flops 1048576 | bytes 8388608 | tf_op jit(solution)/shard_map/mul | solution.py:63
  234.6 57.0 %scatter_fusion = f32[8192,128]{1,0:T(8,128)} fusion(f32[8192,128]{1,0:T(8,128)} %scatter_custom_fusion, s32[8192]{0:T(1024)S(1)} %bitcast.27, f32[8192,128]{1,0:T(8,128)} %bitcast.22), kind=kCustom, calls=%fused_computation.3 | custom fusion | flops 1048576 | bytes 12615680 | tf_op jit(solution)/shard_map/scatter-add | solution.py:63
  (5 shorter events, 0.1 us)
Async XLA Ops:
  6.5 116.0 %copy-start = (f32[1024,128]{1,0:T(8,128)S(1)}, f32[1024,128]{1,0:T(8,128)}, u32[]{:S(2)}) copy-start(f32[1024,128]{1,0:T(8,128)} %param.11) | copy-start | bytes 1572868
  6.5 4.5 %copy-start.1 = (s32[4096,1]{0,1:T(1,128)S(1)}, s32[4096,1]{0,1:T(1,128)}, u32[]{:S(2)}) copy-start(s32[4096,1]{0,1:T(1,128)} %param.9) | copy-start | bytes 49156
  38.3 17.3 %all-to-all-start = ((s32[4,8,256]{2,1,0:T(8,128)}), s32[4,8,256]{2,1,0:T(8,128)S(1)}, u32[]{:S(2)}, u32[]{:S(2)}) async-start(s32[4,8,256]{2,1,0:T(8,128)} %reshape.61), calls=%async_computation.1 | async-start | bytes 65536 | tf_op jit(solution)/shard_map/all_to_all | solution.py:55
  55.6 51.7 %all-to-all-start.2 = ((f32[4,8,256,128]{3,2,1,0:T(8,128)}), f32[4,8,256,128]{3,2,1,0:T(8,128)}, u32[]{:S(2)}, u32[]{:S(2)}) async-start(f32[4,8,256,128]{3,2,1,0:T(8,128)} %bitcast.23), calls=%async_computation.3 | async-start | bytes 8388608 | tf_op jit(solution)/shard_map/all_to_all | solution.py:48
  107.3 10.6 %all-to-all-start.1 = ((s32[4,8,256]{2,0,1:T(4,128)}), s32[4,8,256]{2,0,1:T(4,128)S(1)}, u32[]{:S(2)}, u32[]{:S(2)}) async-start(s32[4,8,256]{2,0,1:T(4,128)} %copy.13), calls=%async_computation.2 | async-start | bytes 65536 | tf_op jit(solution)/shard_map/all_to_all | solution.py:54
  116.7 5.8 %copy-start.2 = (s32[1024]{0:T(1024)S(1)}, s32[1024]{0:T(1024)}, u32[]{:S(2)}) copy-start(s32[1024]{0:T(1024)} %param.12) | copy-start | bytes 12292
  116.7 7.2 %copy-start.3 = (s32[256]{0:T(256)S(1)}, s32[256]{0:T(256)}, u32[]{:S(2)}) copy-start(s32[256]{0:T(256)} %param.13) | copy-start | bytes 3076
  117.9 112.0 %all-to-all-start.3 = ((f32[4,8,256,128]{3,2,0,1:T(8,128)}), f32[4,8,256,128]{3,2,0,1:T(8,128)}, u32[]{:S(2)}, u32[]{:S(2)}) async-start(f32[4,8,256,128]{3,2,0,1:T(8,128)} %copy.15), calls=%async_computation.4 | async-start | bytes 8388608 | tf_op jit(solution)/shard_map/all_to_all | solution.py:47
  122.4 34.8 %reduce-scatter.2.cloned.1.call-start = ((), (), s32[]{:S(2)}) async-start(), calls=%async_computation.5 | async-start | bytes 147456 | tf_op jit(solution)/shard_map/reduce_scatter | solution.py:15
Sparse Core Ops, SparseCore 0:
  125.5 31.7 reduce-scatter.1
where the time goes:
time: 299 us; the launch traced here: 298 us
  waiting for transfers between devices  80.7 us (27%)
  other arithmetic  77.8 us (26%)
  blocking collectives  66.6 us (22%)
  local copies, waits for them, and re-layouts  39.9 us (13%)
  starting transfers between devices  18.6 us (6%)
  between operations  13.5 us (5%)
    scatter-add x1, other arithmetic, on_device(): current.at[got_rows.reshape(-1)].add(-LEARN * got_grads.reshape(-1, width))  57 us
    all_gather x1, blocking collectives, hot_update(): total = lax.all_gather(share, 'dev', axis=0, tiled=True)  50.9 us
    all_to_all x1, waiting for transfers between devices, on_device(): lax.all_to_all(grads_four, 'grp', split_axis=0, concat_axis=0, tiled=True)  46.2 us
    reduce_scatter x1, waiting for transfers between devices, hot_update(): lax.psum_scatter(partial_sum, 'dev', scatter_dimension=0, tiled=True)  33.3 us
    scatter x1, local copies, waits for them, and re-layouts, pack_cold(): jnp.zeros((devices * slots,), jnp.int32).at[target].set(cold_row)  15.7 us
    psum x1, blocking collectives, hot_update(): share = lax.psum(share, 'grp')  15.7 us
    scatter x1, local copies, waits for them, and re-layouts, pack_cold(): jnp.zeros((devices * slots, width), jnp.float32).at[target].set(cold_grads)  13.1 us
    another operation x2, other arithmetic  9.41 us
  transfers between devices with their start and end apart: 5, of which 3 were waited for; matrix products, arithmetic and copies ran while one was open for 9% of the time, Pallas kernels for 0%

commit v1 on v0

--- a/solution.py
+++ b/solution.py
@@ -44,12 +44,20 @@
     grads_four = send_grads.reshape(n_grp, n_dev, slots, width)
     rows_three = send_rows.reshape(n_grp, n_dev, slots)
     got_grads, got_rows = (
-        lax.all_to_all(
-            lax.all_to_all(grads_four, "grp", split_axis=0, concat_axis=0, tiled=True),
-            "dev",
-            split_axis=1,
-            concat_axis=1,
-            tiled=True,
+        jnp.concatenate(
+            lax.all_to_all(
+                jnp.stack(
+                    jnp.split(
+                        lax.all_to_all(grads_four, "grp", split_axis=0, concat_axis=0, tiled=True),
+                        lax.axis_size("dev"),
+                        axis=1,
+                    )
+                ),
+                "dev",
+                0,
+                0,
+            ),
+            axis=1,
         ),
         lax.all_to_all(
             lax.all_to_all(rows_three, "grp", split_axis=0, concat_axis=0, tiled=True),

time: 299 us -> 310 us (1.037)
  local copies, waits for them, and re-layouts: 39.9 us -> 52.7 us
    unnamed x9 -> x16, local copies, waits for them, and re-layouts: 4.56 us -> 17.7 us
    all_to_all x1 -> x0, local copies, waits for them, and re-layouts: 4.57 us -> none  [on_device(): lax.all_to_all(grads_four, 'grp', split_axis=0, concat_axis=0, tiled=True)]
  transfers between devices with their start and end apart: 5 -> 5, of which waited for: 3 -> 2; matrix products, arithmetic and copies ran while one was open for 9% -> 12% of each run, Pallas kernels for 0% -> 0%
where the time goes in v1:
time: 310 us; the launch traced here: 309 us
  waiting for transfers between devices  79.6 us (26%)
  other arithmetic  75.6 us (24%)
  blocking collectives  66.7 us (22%)
  local copies, waits for them, and re-layouts  52.7 us (17%)
  starting transfers between devices  19.2 us (6%)
  between operations  13.5 us (4%)
    scatter-add x1, other arithmetic, on_device(): current.at[got_rows.reshape(-1)].add(-LEARN * got_grads.reshape(-1, width))  57 us
    all_gather x1, blocking collectives, hot_update(): total = lax.all_gather(share, 'dev', axis=0, tiled=True)  51 us
    all_to_all x1, waiting for transfers between devices, on_device(): lax.all_to_all(grads_four, 'grp', split_axis=0, concat_axis=0, tiled=True)  46.2 us
    reduce_scatter x1, waiting for transfers between devices, hot_update(): lax.psum_scatter(partial_sum, 'dev', scatter_dimension=0, tiled=True)  33.3 us
    unnamed x16, local copies, waits for them, and re-layouts  17.7 us
    scatter x1, local copies, waits for them, and re-layouts, pack_cold(): jnp.zeros((devices * slots,), jnp.int32).at[target].set(cold_row)  15.7 us
    psum x1, blocking collectives, hot_update(): share = lax.psum(share, 'grp')  15.7 us
    scatter x1, local copies, waits for them, and re-layouts, pack_cold(): jnp.zeros((devices * slots, width), jnp.float32).at[target].set(cold_grads)  13.1 us
  transfers between devices with their start and end apart: 5, of which 2 were waited for; matrix products, arithmetic and copies ran while one was open for 12% of the time, Pallas kernels for 0%

profile of v1, /device:TPU:4, one launch (start us, length us, event | category | flops | bytes accessed | tf_op | source)
XLA Modules:
  0.0 308.7 jit_solution(2356779726733863759)
XLA Ops:
  6.5 0.0 copy-start
  6.5 0.0 copy-start.1
  6.5 4.5 %copy.67 = f32[8192,128]{1,0:T(8,128)} copy(f32[8192,128]{1,0:T(8,128)} %param.7) | data formatting | bytes 8388608
  11.1 0.0 copy-done.1
  11.1 0.1 fusion.14
  11.1 9.2 %reduce-window.6 = s32[32,32,128]{2,1,0:T(8,128)S(1)} reduce-window(s32[32,32,128]{2,1,0:T(8,128)S(1)} %fusion.14, s32[]{:T(128)} %constant.13.clone.1), window={size=1x1x128 pad=0_0x0_0x127_0}, to_apply=%region_3.4 | reduce-window | flops 16646144 | bytes 1048580 | tf_op jit(solution)/shard_map/reduce-window
  20.4 0.8 slice_reduce_fusion
  21.2 0.2 reduce-window.9
  21.4 0.2 add_add_fusion
  21.6 0.3 fusion.4
  21.9 15.7 %scatter_custom_fusion.1 = s32[8192]{0:T(1024)S(1)} fusion(s32[4096]{0:T(1024)S(1)} %bitcast.80, s32[4096]{0:T(1024)} %param.10, s32[]{:T(128)} %constant.13.clone.1), kind=kCustom, calls=%fused_computation.39 | custom fusion | bytes 33280 | tf_op jit(solution)/shard_map/scatter | solution.py:33
  37.7 0.6 reshape.61
  38.3 4.2 %all-to-all-start = ((s32[4,8,256]{2,1,0:T(8,128)}), s32[4,8,256]{2,1,0:T(8,128)S(1)}, u32[]{:S(2)}, u32[]{:S(2)}) async-start(s32[4,8,256]{2,1,0:T(8,128)} %reshape.61), calls=%async_computation.1 | async-start | bytes 65536 | tf_op jit(solution)/shard_map/all_to_all | solution.py:63
  42.5 13.1 %scatter_custom_fusion.2 = f32[8192,128]{1,0:T(8,128)} fusion(s32[4096]{0:T(1024)S(1)} %bitcast.81, f32[4096,128]{1,0:T(8,128)} %param.8, f32[]{:T(128)} %constant.17.clone.1), kind=kCustom, calls=%fused_computation.5 | custom fusion | bytes 4194816 | tf_op jit(solution)/shard_map/scatter | solution.py:32
  55.6 0.0 all-to-all-done
  55.6 4.8 %all-to-all-start.2 = ((f32[4,8,256,128]{3,2,1,0:T(8,128)}), f32[4,8,256,128]{3,2,1,0:T(8,128)}, u32[]{:S(2)}, u32[]{:S(2)}) async-start(f32[4,8,256,128]{3,2,1,0:T(8,128)} %bitcast.73), calls=%async_computation.3 | async-start | bytes 8388608 | tf_op jit(solution)/shard_map/all_to_all | solution.py:51
  60.5 0.6 copy.38
  61.1 46.2 %all-to-all-done.2 = f32[4,8,256,128]{3,2,1,0:T(8,128)} async-done(((f32[4,8,256,128]{3,2,1,0:T(8,128)}), f32[4,8,256,128]{3,2,1,0:T(8,128)}, u32[]{:S(2)}, u32[]{:S(2)}) %all-to-all-start.2) | async-done | bytes 4194336 | tf_op jit(solution)/shard_map/all_to_all | solution.py:51
  107.3 4.9 %all-to-all-start.1 = ((s32[4,8,256]{2,0,1:T(4,128)}), s32[4,8,256]{2,0,1:T(4,128)S(1)}, u32[]{:S(2)}, u32[]{:S(2)}) async-start(s32[4,8,256]{2,0,1:T(4,128)} %copy.38), calls=%async_computation.2 | async-start | bytes 65536 | tf_op jit(solution)/shard_map/all_to_all | solution.py:62
  112.2 1.9 fusion.12
  114.1 1.9 fusion.11
  116.0 1.9 fusion.10
  117.8 1.9 fusion.9
  119.7 1.9 fusion.8
  121.6 1.9 fusion.7
  123.5 1.9 fusion.6
  125.4 1.9 fusion.5
  127.3 0.0 copy-start.2
  127.3 0.0 copy-start.3
  127.3 0.0 all-to-all-done.1
  127.3 5.2 %all-to-all-start.3 = ((f32[8,4,1,256,128]{4,3,1,2,0:T(8,128)}), f32[8,4,1,256,128]{4,3,1,2,0:T(8,128)}, u32[]{:S(2)}, u32[]{:S(2)}) async-start(f32[8,4,1,256,128]{4,3,1,2,0:T(8,128)} %fusion.5), calls=%async_computation.4 | async-start | bytes 8388608 | tf_op jit(solution)/shard_map/all_to_all | solution.py:48
  132.5 0.0 reduce-scatter.2.cloned.1.call-start
  132.5 0.0 copy-done
  132.6 0.0 copy-done.2
  132.6 1.3 fusion.2
  133.9 0.0 reduce-scatter.2.cloned.1.call-update
  133.9 0.0 copy-done.3
  134.1 33.3 %reduce-scatter.2.cloned.1.call-done = f32[32,128]{1,0:T(8,128)} async-done(((f32[256,128]{1,0:T(8,128)}), f32[32,128]{1,0:T(8,128)}) %reduce-scatter.2.cloned.1.call-update) | async-done | bytes 16400 | tf_op jit(solution)/shard_map/reduce_scatter | solution.py:15
  167.4 15.7 %psum.7 = f32[32,128]{1,0:T(8,128)S(1)} all-reduce(f32[32,128]{1,0:T(8,128)} %reduce-scatter.2.cloned.1.call-done), channel_id=1, replica_groups=mesh['grp'=4,'dev'=8] {'grp'}, use_global_device_ids=true, to_apply=%region_1.2 | all-reduce | flops 4096 | bytes 32768 | tf_op jit(solution)/shard_map/psum | solution.py:16
  183.1 51.0 %all_gather.3 = f32[256,128]{1,0:T(8,128)S(1)} all-gather(f32[32,128]{1,0:T(8,128)S(1)} %psum.7), channel_id=1, replica_groups=mesh['grp'=4,'dev'=8] {'dev'}, dimensions={0}, use_global_device_ids=true | all-gather | bytes 147456 | tf_op jit(solution)/shard_map/all_gather | solution.py:17
  234.1 6.0 %scatter_custom_fusion = f32[8192,128]{1,0:T(8,128)} fusion(f32[8192,128]{1,0:T(8,128)} %copy.67, s32[256]{0:T(256)S(1)} %compare_select_fusion.2, f32[256,128]{1,0:T(8,128)S(1)} %all_gather.3, f32[]{:T(128)} %constant.14.clone.1), kind=kCustom, calls=%fused_computation.35 | custom fusion | flops 65536 | bytes 4325888 | tf_op jit(solution)/shard_map/scatter-add | solution.py:22
  240.1 0.0 all-to-all-done.3
  240.1 2.6 multiply_bitcast_fusion
  242.6 2.2 copy.47
  244.8 57.0 %scatter_fusion = f32[8192,128]{1,0:T(8,128)} fusion(f32[8192,128]{1,0:T(8,128)} %scatter_custom_fusion, s32[8192]{0:T(1024)S(1)} %bitcast.77, f32[8192,128]{1,0:T(8,128)} %bitcast.72), kind=kCustom, calls=%fused_computation.3 | custom fusion | flops 1048576 | bytes 12615680 | tf_op jit(solution)/shard_map/scatter-add | solution.py:71
  (5 shorter events, 0.1 us)
Async XLA Ops:
  6.5 126.0 %copy-start = (f32[1024,128]{1,0:T(8,128)S(1)}, f32[1024,128]{1,0:T(8,128)}, u32[]{:S(2)}) copy-start(f32[1024,128]{1,0:T(8,128)} %param.11) | copy-start | bytes 1572868
  6.5 4.5 %copy-start.1 = (s32[4096,1]{0,1:T(1,128)S(1)}, s32[4096,1]{0,1:T(1,128)}, u32[]{:S(2)}) copy-start(s32[4096,1]{0,1:T(1,128)} %param.9) | copy-start | bytes 49156
  38.3 17.3 %all-to-all-start = ((s32[4,8,256]{2,1,0:T(8,128)}), s32[4,8,256]{2,1,0:T(8,128)S(1)}, u32[]{:S(2)}, u32[]{:S(2)}) async-start(s32[4,8,256]{2,1,0:T(8,128)} %reshape.61), calls=%async_computation.1 | async-start | bytes 65536 | tf_op jit(solution)/shard_map/all_to_all | solution.py:63
  55.6 51.7 %all-to-all-start.2 = ((f32[4,8,256,128]{3,2,1,0:T(8,128)}), f32[4,8,256,128]{3,2,1,0:T(8,128)}, u32[]{:S(2)}, u32[]{:S(2)}) async-start(f32[4,8,256,128]{3,2,1,0:T(8,128)} %bitcast.73), calls=%async_computation.3 | async-start | bytes 8388608 | tf_op jit(solution)/shard_map/all_to_all | solution.py:51
  107.3 19.9 %all-to-all-start.1 = ((s32[4,8,256]{2,0,1:T(4,128)}), s32[4,8,256]{2,0,1:T(4,128)S(1)}, u32[]{:S(2)}, u32[]{:S(2)}) async-start(s32[4,8,256]{2,0,1:T(4,128)} %copy.38), calls=%async_computation.2 | async-start | bytes 65536 | tf_op jit(solution)/shard_map/all_to_all | solution.py:62
  127.3 5.3 %copy-start.2 = (s32[1024]{0:T(1024)S(1)}, s32[1024]{0:T(1024)}, u32[]{:S(2)}) copy-start(s32[1024]{0:T(1024)} %param.12) | copy-start | bytes 12292
  127.3 6.7 %copy-start.3 = (s32[256]{0:T(256)S(1)}, s32[256]{0:T(256)}, u32[]{:S(2)}) copy-start(s32[256]{0:T(256)} %param.13) | copy-start | bytes 3076
  127.3 112.8 %all-to-all-start.3 = ((f32[8,4,1,256,128]{4,3,1,2,0:T(8,128)}), f32[8,4,1,256,128]{4,3,1,2,0:T(8,128)}, u32[]{:S(2)}, u32[]{:S(2)}) async-start(f32[8,4,1,256,128]{4,3,1,2,0:T(8,128)} %fusion.5), calls=%async_computation.4 | async-start | bytes 8388608 | tf_op jit(solution)/shard_map/all_to_all | solution.py:48
  132.5 34.9 %reduce-scatter.2.cloned.1.call-start = ((), (), s32[]{:S(2)}) async-start(), calls=%async_computation.5 | async-start | bytes 147456 | tf_op jit(solution)/shard_map/reduce_scatter | solution.py:15
Sparse Core Ops, SparseCore 0:
  135.5 31.7 reduce-scatter.1
